TPU v7x, 32 devices: a whole 2x2x4 slice. The times are simulated.
32 devices in a mesh: seq: 16 (over z, y, core), res: 2 (over x).
Axes of the slice: x: 2, y: 2, z: 4, core: 2. Of those that a mesh axis runs over, the one named last changes fastest.
Arguments:
- homolog_embedding: bfloat16 [256, 128, 256], P('seq', 'res'), may hold values from -6 to 6
- pair_features: bfloat16 [128, 128, 128], P('seq', 'res'), may hold values from -6 to 6
- row_present_mask: int32 [256], replicated, may hold values 0 or 1
- residue_keep_mask: int32 [128], replicated, may hold values 0 or 1
- query_weight: bfloat16 [256, 256], replicated, may hold values from -64 to 64
- key_weight: bfloat16 [256, 256], replicated, may hold values from -1 to 1
- content_matrix: bfloat16 [256, 256], replicated, may hold values from -0.375 to 0.375
- sigmoid_switch_matrix: bfloat16 [256, 256], replicated, may hold values from -0.375 to 0.375
- focus_merge_matrix: bfloat16 [256, 256], replicated, may hold values from -0.375 to 0.375
- widening_matrix: bfloat16 [256, 1024], replicated, may hold values from -0.375 to 0.375
- narrowing_matrix: bfloat16 [1024, 256], replicated, may hold values from -0.1875 to 0.1875
- first_factor_matrix: bfloat16 [256, 32], replicated, may hold values from -0.375 to 0.375
- second_factor_matrix: bfloat16 [256, 32], replicated, may hold values from -0.375 to 0.375
- outer_product_weight: bfloat16 [1024, 128], replicated, may hold values from -1 to 1
- outer_product_bias: float32 [128], replicated, may hold values from -3 to 3
- pair_up_weight: bfloat16 [128, 512], replicated, may hold values from -0.5 to 0.5
- pair_down_weight: bfloat16 [512, 128], replicated, may hold values from -0.25 to 0.25
Outputs:
- msa_update: bfloat16 [256, 128, 256], P('seq', 'res')
- pair_update: bfloat16 [128, 128, 128], P('seq', 'res')
All inputs are finite; a program needn't handle non-finite values.
Results may differ from a plain program's by a relative error of at most 0.012.
Values may be sent and summed in bfloat16 or wider, within the bound.
A program may use at most 64 MiB of HBM per device.

v0:
```python
import math
import jax
import jax.numpy as jnp
from jax import lax
from jax.sharding import PartitionSpec as P

FOCUS_NUMBER = 8
FOCUS_BREADTH = 32
COUPLING_DIM = 32
epsilon = 1e-05
mask_fill = 1000000000.0


def layer_norm(values):
    centre = values - jnp.mean(values, axis=-1, keepdims=True)
    spread = jnp.mean(centre * centre, axis=-1, keepdims=True)
    return centre * lax.rsqrt(spread + epsilon)


def column_delta(block, row_present_flags, attention_weights):
    (
        query_weight,
        key_weight,
        content_matrix,
        sigmoid_switch_matrix,
        focus_merge_matrix,
        widening_matrix,
        narrowing_matrix,
        first_factor_matrix,
        second_factor_matrix,
    ) = attention_weights
    row_count, item_count, channel_width = block.shape
    inputs = block.astype(jnp.float32)
    normed = layer_norm(inputs).astype(jnp.bfloat16)
    scaling = 1.0 / math.sqrt(FOCUS_BREADTH)
    queries = (jnp.dot(normed, query_weight, preferred_element_type=jnp.float32) * scaling).astype(
        jnp.bfloat16
    )
    queries = queries.reshape(row_count, item_count, FOCUS_NUMBER, FOCUS_BREADTH)
    keys_all = jnp.dot(normed, key_weight, preferred_element_type=jnp.float32).astype(jnp.bfloat16)
    keys_all = keys_all.reshape(row_count, item_count, FOCUS_NUMBER, FOCUS_BREADTH)
    values_all = jnp.dot(normed, content_matrix, preferred_element_type=jnp.float32).astype(
        jnp.bfloat16
    )
    values_all = values_all.reshape(row_count, item_count, FOCUS_NUMBER, FOCUS_BREADTH)
    gate_values = jax.nn.sigmoid(
        jnp.dot(normed, sigmoid_switch_matrix, preferred_element_type=jnp.float32)
    )
    scores = jnp.einsum("skhd,tkhd->khst", queries, keys_all, preferred_element_type=jnp.float32)
    scores = scores + ((row_present_flags - 1.0) * mask_fill)[None, None, None, :]
    peak_score = jnp.max(scores, axis=-1, keepdims=True)
    exponent = jnp.exp(scores - peak_score)
    probs = (exponent / jnp.sum(exponent, axis=-1, keepdims=True)).astype(jnp.bfloat16)
    attended = jnp.einsum("khst,tkhd->skhd", probs, values_all, preferred_element_type=jnp.float32)
    attended = attended.reshape(row_count, item_count, FOCUS_NUMBER * FOCUS_BREADTH)
    gated = (gate_values * attended).astype(jnp.bfloat16)
    after_attn = (
        inputs + jnp.dot(gated, focus_merge_matrix, preferred_element_type=jnp.float32)
    ).astype(jnp.bfloat16)
    normed_two = layer_norm(after_attn.astype(jnp.float32)).astype(jnp.bfloat16)
    hidden = jax.nn.relu(
        jnp.dot(normed_two, widening_matrix, preferred_element_type=jnp.float32)
    ).astype(jnp.bfloat16)
    after_trans = (
        after_attn.astype(jnp.float32)
        + jnp.dot(hidden, narrowing_matrix, preferred_element_type=jnp.float32)
    ).astype(jnp.bfloat16)
    normed_three = layer_norm(after_trans.astype(jnp.float32)).astype(jnp.bfloat16)
    row_scale = row_present_flags[:, None, None]
    left_proj = (
        jnp.dot(normed_three, first_factor_matrix, preferred_element_type=jnp.float32) * row_scale
    ).astype(jnp.bfloat16)
    right_proj = (
        jnp.dot(normed_three, second_factor_matrix, preferred_element_type=jnp.float32) * row_scale
    ).astype(jnp.bfloat16)
    return (after_trans, left_proj, right_proj)


def pair_block_update(
    left_rows,
    right_full,
    pair_block,
    norm_block,
    outer_product_weight,
    outer_product_bias,
    pair_up_weight,
    pair_down_weight,
):
    outer = jnp.einsum(
        "sic,sje->ijce", left_rows, right_full, preferred_element_type=jnp.float32
    ).astype(jnp.bfloat16)
    row_span, column_extent = norm_block.shape
    flat = outer.reshape(row_span, column_extent, COUPLING_DIM * COUPLING_DIM)
    projected = (
        jnp.dot(flat, outer_product_weight, preferred_element_type=jnp.float32) + outer_product_bias
    )
    outer_mean = projected / jnp.maximum(norm_block, 1.0)[:, :, None]
    pair_mid = (pair_block.astype(jnp.float32) + outer_mean).astype(jnp.bfloat16)
    normed = layer_norm(pair_mid.astype(jnp.float32)).astype(jnp.bfloat16)
    hidden = jax.nn.relu(
        jnp.dot(normed, pair_up_weight, preferred_element_type=jnp.float32)
    ).astype(jnp.bfloat16)
    return (
        pair_mid.astype(jnp.float32)
        + jnp.dot(hidden, pair_down_weight, preferred_element_type=jnp.float32)
    ).astype(jnp.bfloat16)


def per_device(
    homolog_embedding,
    pair_features,
    row_present_mask,
    residue_keep_mask,
    query_weight,
    key_weight,
    content_matrix,
    sigmoid_switch_matrix,
    focus_merge_matrix,
    widening_matrix,
    narrowing_matrix,
    first_factor_matrix,
    second_factor_matrix,
    outer_product_weight,
    outer_product_bias,
    pair_up_weight,
    pair_down_weight,
):
    seq_count = lax.axis_size("seq")
    res_count = lax.axis_size("res")
    seq_index = lax.axis_index("seq")
    res_index = lax.axis_index("res")
    shard_rows, column_extent, channel_width = homolog_embedding.shape
    residue_total = column_extent * res_count
    row_span = residue_total // seq_count
    owned_columns = column_extent // seq_count
    row_present_flags = row_present_mask.astype(jnp.float32)
    attention_weights = (
        query_weight,
        key_weight,
        content_matrix,
        sigmoid_switch_matrix,
        focus_merge_matrix,
        widening_matrix,
        narrowing_matrix,
        first_factor_matrix,
        second_factor_matrix,
    )
    grouped = homolog_embedding.reshape(shard_rows, seq_count, owned_columns, channel_width)
    flat_block = lax.all_to_all(grouped, "seq", split_axis=1, concat_axis=0, tiled=True)[:, 0]
    after_trans, left_proj, right_proj = column_delta(
        flat_block, row_present_flags, attention_weights
    )
    alignment_columns = after_trans[:, None]
    left_column_set = left_proj[:, None]
    right_column_set = right_proj[:, None]
    alignment_columns = alignment_columns[:, 0]
    left_column_set = left_column_set[:, 0]
    right_column_set = right_column_set[:, 0]
    alignment_output, left_home = (
        lax.all_to_all(alignment_columns, "seq", split_axis=0, concat_axis=1, tiled=True),
        lax.all_to_all(left_column_set, "seq", split_axis=0, concat_axis=1, tiled=True),
    )
    right_full = lax.all_gather(right_column_set, "seq", axis=1, tiled=True)
    left_wide = lax.all_gather(left_home, "res", axis=1, tiled=True)
    left_rows = lax.all_to_all(left_wide, "seq", split_axis=1, concat_axis=0, tiled=True)
    row_res = lax.dynamic_slice_in_dim(residue_keep_mask, seq_index * row_span, row_span, 0)
    col_res = lax.dynamic_slice_in_dim(
        residue_keep_mask, res_index * column_extent, column_extent, 0
    )
    left_rows = left_rows * row_res.astype(jnp.bfloat16)[None, :, None]
    right_full = right_full * col_res.astype(jnp.bfloat16)[None, :, None]
    live_rows = jnp.sum(row_present_flags)
    norm_tile = (
        live_rows * row_res.astype(jnp.float32)[:, None] * col_res.astype(jnp.float32)[None, :]
    )
    overall_rows = left_rows.shape[0]
    block_rows = math.gcd(row_span, 8)
    block_count = row_span // block_rows
    left_groups = left_rows.reshape(overall_rows, block_count, block_rows, COUPLING_DIM).transpose(
        1, 0, 2, 3
    )
    pair_groups = pair_features.reshape(
        block_count, block_rows, column_extent, pair_features.shape[2]
    )
    norm_groups = norm_tile.reshape(block_count, block_rows, column_extent)

    def per_rows(pieces):
        left_block, pair_block, norm_block = pieces
        return pair_block_update(
            left_block,
            right_full,
            pair_block,
            norm_block,
            outer_product_weight,
            outer_product_bias,
            pair_up_weight,
            pair_down_weight,
        )

    pair_output = lax.map(per_rows, (left_groups, pair_groups, norm_groups))
    pair_output = pair_output.reshape(row_span, column_extent, pair_features.shape[2])
    return (alignment_output, pair_output)


def solution(mesh):
    placed = (
        P("seq", "res", None),
        P("seq", "res", None),
        P(),
        P(),
        P(),
        P(),
        P(),
        P(),
        P(),
        P(),
        P(),
        P(),
        P(),
        P(),
        P(),
        P(),
        P(),
    )
    return jax.shard_map(
        per_device,
        mesh=mesh,
        in_specs=placed,
        out_specs=(P("seq", "res", None), P("seq", "res", None)),
        check_vma=False,
    )
```

profile of v0, /device:TPU:0, one launch (start us, length us, event | category | flops | bytes accessed | tf_op | source)
XLA Modules:
  0.0 129.4 jit_solution(13391735593208518622)
XLA Ops:
  7.2 2.2 %copy.150 = bf16[16,64,256]{2,0,1:T(8,128)(2,1)} copy(bf16[16,64,256]{2,1,0:T(8,128)(2,1)} %param.17) | data formatting | bytes 1048576 | tf_op args[0]
  9.4 7.4 %all-to-all-start = ((bf16[16,16,4,256]{3,0,2,1:T(8,128)(2,1)}), bf16[16,16,4,256]{3,0,2,1:T(8,128)(2,1)S(1)}, u32[]{:S(2)}, u32[]{:S(2)}) async-start(bf16[16,16,4,256]{3,0,2,1:T(8,128)(2,1)} %bitcast), calls=%async_computation | async-start | bytes 1048576 | tf_op jit(solution)/shard_map/all_to_all | solution.py:149
  16.8 0.7 convert_element_type.120
  17.5 1.3 %convert_reduce_fusion.2 = (f32[]{:T(128)}, f32[256]{0:T(256)S(1)}) fusion(s32[256]{0:T(256)} %param.19), kind=kLoop, calls=%fused_computation.96 | loop fusion | flops 1023 | bytes 2052 | tf_op jit(solution)/shard_map/reduce_sum | solution.py:172
  18.9 12.2 %all-to-all-done = bf16[16,16,4,256]{3,0,2,1:T(8,128)(2,1)S(1)} async-done(((bf16[16,16,4,256]{3,0,2,1:T(8,128)(2,1)}), bf16[16,16,4,256]{3,0,2,1:T(8,128)(2,1)S(1)}, u32[]{:S(2)}, u32[]{:S(2)}) %all-to-all-start) | async-done | bytes 524320 | tf_op jit(solution)/shard_map/all_to_all | solution.py:149
  31.1 0.2 fusion.39
  31.3 0.1 div.52
  31.4 0.4 multiply_reduce_fusion
  31.9 0.1 rsqrt.37
  32.0 0.1 convert_bitcast_fusion.1
  32.1 0.1 copy.151
  32.2 0.3 copy.161
  32.5 0.3 multiply_convert_fusion
  32.9 0.3 convolution_convert_fusion
  33.3 1.1 fusion.14
  34.4 0.3 convolution_convert_fusion.1
  34.8 7.0 %fusion.74 = (f32[4,8,256]{2,1,0:T(8,128)S(1)}, f32[4,8,256,256]{2,3,1,0:T(8,128)}) fusion(f32[256]{0:T(256)S(1)} %get-tuple-element.43, bf16[256,4,8,32]{0,3,2,1:T(8,128)(2,1)} %bitcast.120, bf16[256,4,8,32]{0,3,2,1:T(8,128)(2,1)S(1)} %bitcast.119), kind=kOutput, calls=%fused_computation.100 | convolution fusion | flops 140509440 | bytes 9470976 | tf_op jit(solution)/shard_map/sub | solution.py:52
  41.8 5.3 %fusion.5 = f32[4,8,32,256]{3,2,1,0:T(8,128)} fusion(bf16[256,4,8,32]{0,3,2,1:T(8,128)(2,1)S(1)} %bitcast.118, f32[4,8,256,256]{2,3,1,0:T(8,128)} %get-tuple-element.47, f32[4,8,256]{2,1,0:T(8,128)S(1)} %get-tuple-element.46), kind=kOutput, calls=%fused_computation.8 | convolution fusion | flops 138412032 | bytes 9994240 | tf_op jit(solution)/shard_map/khst,tkhd->skhd/dot_general | solution.py:54
  47.1 1.6 %copy.159 = f32[256,4,256]{2,0,1:T(8,128)S(1)} copy(f32[256,4,256]{0,2,1:T(8,128)} %bitcast.116) | data formatting | bytes 2097152 | tf_op jit(solution)/shard_map/reshape | solution.py:55
  48.7 1.4 %convert_reduce_fusion = (f32[256,4]{0,1:T(4,128)S(1)}, bf16[256,4,256]{0,2,1:T(8,128)(2,1)}) fusion(f32[256,4,256]{0,2,1:T(8,128)S(1)} %copy.161, bf16[256,256]{1,0:T(8,128)(2,1)S(1)} %copy-done.6, f32[256,4,256]{2,0,1:T(8,128)S(1)} %copy.159, bf16[256,4,256]{2,0,1:T(8,128)(2,1)S(1)} %multiply_convert_fusion, bf16[256,256]{1,0:T(8,128)(2,1)S(1)} %copy-done.7), kind=kOutput, calls=%fused_computation.12 | convolution fusion | flops 270793728 | bytes 3411968 | tf_op jit(solution)/shard_map/dot_general | solution.py:58
  50.1 1.2 fusion.29
  51.4 2.7 %convert_reduce_fusion.1 = (f32[256,4]{0,1:T(4,128)S(1)}, bf16[256,4,256]{0,2,1:T(8,128)(2,1)S(1)}) fusion(bf16[1024,256]{1,0:T(8,128)(2,1)S(1)} %copy-done, bf16[256,4,256]{0,2,1:T(8,128)(2,1)} %get-tuple-element.49, bf16[256,1024]{1,0:T(8,128)(2,1)} %param.26, f32[256,4]{0,1:T(4,128)S(1)} %add_rsqrt_fusion.2, f32[256,4]{0,1:T(4,128)S(1)} %broadcast_multiply_fusion.2), kind=kOutput, calls=%fused_computation.22 | convolution fusion | flops 1078197248 | bytes 2109440 | tf_op jit(solution)/shard_map/dot_general | solution.py:66
  54.1 0.2 fusion.31
  54.2 0.9 fusion.27
  55.1 0.3 fusion.28
  55.4 0.2 copy.169
  55.6 0.3 reshape.153
  55.9 10.9 %all_to_all.63 = bf16[16,2,1024]{2,1,0:T(2,128)(2,1)S(1)} all-to-all(bf16[16,2,1024]{2,1,0:T(2,128)(2,1)S(1)} %reshape.153), channel_id=1, replica_groups=mesh['seq'=16,'res'=2] {'seq'}, dimensions={0} | all-to-all | bytes 131072 | tf_op jit(solution)/shard_map/all_to_all | solution.py:161
  66.7 0.2 reshape.154
  67.0 8.4 %all_gather.7 = bf16[16,128,32]{2,0,1:T(8,128)(2,1)S(1)} all-gather(bf16[16,64,32]{2,0,1:T(8,128)(2,1)S(1)} %bitcast.115), channel_id=1, replica_groups=mesh['seq'=16,'res'=2] {'res'}, dimensions={1}, use_global_device_ids=true | all-gather | bytes 196608 | tf_op jit(solution)/shard_map/all_gather | solution.py:164
  75.4 1.2 reshape.155
  76.6 3.5 %all-to-all-start.3 = ((bf16[16,2,2048]{2,1,0:T(2,128)(2,1)}), bf16[16,2,2048]{2,1,0:T(2,128)(2,1)S(1)}, u32[]{:S(2)}, u32[]{:S(2)}) async-start(bf16[16,2,2048]{2,1,0:T(2,128)(2,1)} %reshape.155), calls=%async_computation.3 | async-start | bytes 262144 | tf_op jit(solution)/shard_map/all_to_all | solution.py:165
  80.1 1.1 copy.164
  81.2 8.0 %all-to-all-done.3 = bf16[16,2,2048]{2,1,0:T(2,128)(2,1)S(1)} async-done(((bf16[16,2,2048]{2,1,0:T(2,128)(2,1)}), bf16[16,2,2048]{2,1,0:T(2,128)(2,1)S(1)}, u32[]{:S(2)}, u32[]{:S(2)}) %all-to-all-start.3) | async-done | bytes 131104 | tf_op jit(solution)/shard_map/all_to_all | solution.py:165
  89.1 3.8 %all-to-all-start.1 = ((bf16[256,4,256]{2,1,0:T(4,128)(2,1)}), bf16[256,4,256]{2,1,0:T(4,128)(2,1)S(1)}, u32[]{:S(2)}, u32[]{:S(2)}) async-start(bf16[256,4,256]{2,1,0:T(4,128)(2,1)} %copy.164), calls=%async_computation.1 | async-start | bytes 1048576 | tf_op jit(solution)/shard_map/all_to_all | solution.py:160
  92.9 0.1 dynamic-slice_convert_fusion
  93.0 0.7 convert_multiply_fusion
  93.9 0.3 reshape.156
  94.1 0.1 copy.173
  94.3 0.1 bitcast_multiply_fusion
  94.4 0.3 copy.174
  94.7 12.2 %all-to-all-done.1 = bf16[256,4,256]{2,1,0:T(4,128)(2,1)S(1)} async-done(((bf16[256,4,256]{2,1,0:T(4,128)(2,1)}), bf16[256,4,256]{2,1,0:T(4,128)(2,1)S(1)}, u32[]{:S(2)}, u32[]{:S(2)}) %all-to-all-start.1) | async-done | bytes 524320 | tf_op jit(solution)/shard_map/all_to_all | solution.py:160
  107.1 1.0 copy.177
  108.1 4.4 %convert_bitcast_fusion = bf16[8,64,32,32]{2,3,0,1:T(8,128)(2,1)} fusion(bf16[256,64,32]{0,2,1:T(8,128)(2,1)} %all-gather.2.cloned.1.call-done, bf16[64]{0:T(256)(128)(2,1)S(1)} %get-tuple-element.45, bf16[256,8,32]{0,2,1:T(8,128)(2,1)S(1)} %copy.174), kind=kOutput, calls=%fused_computation.5 | convolution fusion | flops 271056896 | bytes 2228352 | tf_op jit(solution)/shard_map/while/body/eval_jaxpr/sic,sje->ijce/dot_general | solution.py:89
  112.5 7.7 %copy.175 = bf16[8,64,32,32]{1,3,2,0:T(8,128)(2,1)S(1)} copy(bf16[8,64,32,32]{2,3,0,1:T(8,128)(2,1)} %convert_bitcast_fusion) | data formatting | bytes 2097152 | tf_op jit(solution)/shard_map/while/body/eval_jaxpr/convert_element_type | solution.py:91
  120.3 0.8 fusion.81
  121.1 0.3 multiply_reduce_fusion.1
  121.4 1.2 fusion.26
  (46 shorter events, 0.5 us)
Async XLA Ops:
  7.2 44.2 %copy-start = (bf16[1024,256]{1,0:T(8,128)(2,1)S(1)}, bf16[1024,256]{1,0:T(8,128)(2,1)}, u32[]{:S(2)}) copy-start(bf16[1024,256]{1,0:T(8,128)(2,1)} %param.27) | copy-start | bytes 1572868
  9.4 21.7 %all-to-all-start = ((bf16[16,16,4,256]{3,0,2,1:T(8,128)(2,1)}), bf16[16,16,4,256]{3,0,2,1:T(8,128)(2,1)S(1)}, u32[]{:S(2)}, u32[]{:S(2)}) async-start(bf16[16,16,4,256]{3,0,2,1:T(8,128)(2,1)} %bitcast), calls=%async_computation | async-start | bytes 1048576 | tf_op jit(solution)/shard_map/all_to_all | solution.py:149
  16.8 91.3 %all-gather.2.cloned.1.call-start = ((), (), s32[]{:S(2)}) async-start(), calls=%async_computation.4 | async-start | bytes 1114112 | tf_op jit(solution)/shard_map/all_gather | solution.py:163
  31.3 1.6 %copy-start.1 = (bf16[256,256]{1,0:T(8,128)(2,1)S(1)}, bf16[256,256]{1,0:T(8,128)(2,1)}, u32[]{:S(2)}) copy-start(bf16[256,256]{1,0:T(8,128)(2,1)} %param.22) | copy-start | bytes 393220
  32.0 1.3 copy-start.2
  32.1 2.3 %copy-start.3 = (bf16[256,256]{1,0:T(8,128)(2,1)S(1)}, bf16[256,256]{1,0:T(8,128)(2,1)}, u32[]{:S(2)}) copy-start(bf16[256,256]{1,0:T(8,128)(2,1)} %param.23) | copy-start | bytes 393220
  41.8 6.9 %copy-start.6 = (bf16[256,256]{1,0:T(8,128)(2,1)S(1)}, bf16[256,256]{1,0:T(8,128)(2,1)}, u32[]{:S(2)}) copy-start(bf16[256,256]{1,0:T(8,128)(2,1)} %param.25) | copy-start | bytes 393220
  41.8 6.9 %copy-start.7 = (bf16[256,256]{1,0:T(8,128)(2,1)S(1)}, bf16[256,256]{1,0:T(8,128)(2,1)}, u32[]{:S(2)}) copy-start(bf16[256,256]{1,0:T(8,128)(2,1)} %param.24) | copy-start | bytes 393220
  50.1 4.1 %copy-start.11 = (bf16[256,32]{0,1:T(8,128)(2,1)S(1)}, bf16[256,32]{0,1:T(8,128)(2,1)}, u32[]{:S(2)}) copy-start(bf16[256,32]{0,1:T(8,128)(2,1)} %param.29) | copy-start | bytes 49156
  50.1 5.0 %copy-start.12 = (bf16[256,32]{0,1:T(8,128)(2,1)S(1)}, bf16[256,32]{0,1:T(8,128)(2,1)}, u32[]{:S(2)}) copy-start(bf16[256,32]{0,1:T(8,128)(2,1)} %param.28) | copy-start | bytes 49156
  54.0 38.9 %copy-start.4 = (s32[128]{0:T(128)S(1)}, s32[128]{0:T(128)}, u32[]{:S(2)}) copy-start(s32[128]{0:T(128)} %param.20) | copy-start | bytes 1540
  76.6 12.5 %all-to-all-start.3 = ((bf16[16,2,2048]{2,1,0:T(2,128)(2,1)}), bf16[16,2,2048]{2,1,0:T(2,128)(2,1)S(1)}, u32[]{:S(2)}, u32[]{:S(2)}) async-start(bf16[16,2,2048]{2,1,0:T(2,128)(2,1)} %reshape.155), calls=%async_computation.3 | async-start | bytes 262144 | tf_op jit(solution)/shard_map/all_to_all | solution.py:165
  89.1 17.8 %all-to-all-start.1 = ((bf16[256,4,256]{2,1,0:T(4,128)(2,1)}), bf16[256,4,256]{2,1,0:T(4,128)(2,1)S(1)}, u32[]{:S(2)}, u32[]{:S(2)}) async-start(bf16[256,4,256]{2,1,0:T(4,128)(2,1)} %copy.164), calls=%async_computation.1 | async-start | bytes 1048576 | tf_op jit(solution)/shard_map/all_to_all | solution.py:160
  112.5 7.7 %copy-start.5 = (bf16[1024,128]{1,0:T(8,128)(2,1)S(1)}, bf16[1024,128]{1,0:T(8,128)(2,1)}, u32[]{:S(2)}) copy-start(bf16[1024,128]{1,0:T(8,128)(2,1)} %param.30) | copy-start | bytes 786436
  112.5 7.7 %copy-start.8 = (bf16[8,64,128]{2,1,0:T(8,128)(2,1)S(1)}, bf16[8,64,128]{2,1,0:T(8,128)(2,1)}, u32[]{:S(2)}) copy-start(bf16[8,64,128]{2,1,0:T(8,128)(2,1)} %param.18) | copy-start | bytes 393220
  112.5 7.7 %copy-start.13 = (f32[128]{0:T(128)S(1)}, f32[128]{0:T(128)}, u32[]{:S(2)}) copy-start(f32[128]{0:T(128)} %param.31) | copy-start | bytes 1540
  112.5 8.9 %copy-start.9 = (bf16[512,128]{1,0:T(8,128)(2,1)S(1)}, bf16[512,128]{1,0:T(8,128)(2,1)}, u32[]{:S(2)}) copy-start(bf16[512,128]{1,0:T(8,128)(2,1)} %param.33) | copy-start | bytes 393220
  112.5 8.9 %copy-start.10 = (bf16[128,512]{1,0:T(8,128)(2,1)S(1)}, bf16[128,512]{1,0:T(8,128)(2,1)}, u32[]{:S(2)}) copy-start(bf16[128,512]{1,0:T(8,128)(2,1)} %param.32) | copy-start | bytes 393220
Sparse Core Ops, SparseCore 0:
  55.3 37.4 all-gather.1
where the time goes:
time: 130 us; the launch traced here: 129 us
  waiting for transfers between devices  32.4 us (25%)
  matrix products  25.8 us (20%)
  blocking collectives  19.3 us (15%)
  local copies, waits for them, and re-layouts  16.8 us (13%)
  starting transfers between devices  14.7 us (11%)
  between operations  14.4 us (11%)
  other arithmetic  5.9 us (5%)
    all_to_all x1, waiting for transfers between devices, per_device(): lax.all_to_all(alignment_columns, 'seq', split_axis=0, concat_axis=1, til...  12.2 us
    all_to_all x1, waiting for transfers between devices, per_device(): lax.all_to_all(grouped, 'seq', split_axis=1, concat_axis=0, tiled=True)  12.2 us
    all_to_all x1, blocking collectives, per_device(): lax.all_to_all(left_column_set, 'seq', split_axis=0, concat_axis=1, tiled...  10.9 us
    all_gather x1, blocking collectives, per_device(): left_wide = lax.all_gather(left_home, 'res', axis=1, tiled=True)  8.43 us
    all_to_all x1, waiting for transfers between devices, per_device(): lax.all_to_all(left_wide, 'seq', split_axis=1, concat_axis=0, tiled=True)  7.96 us
    convert_element_type x1, local copies, waits for them, and re-layouts, pair_block_update(): outer = jnp.einsum('sic,sje->ijce', left_rows, right_full, preferred_elem...  7.69 us
    all_to_all x1, starting transfers between devices, per_device(): lax.all_to_all(grouped, 'seq', split_axis=1, concat_axis=0, tiled=True)  7.41 us
    sub x1, matrix products, column_delta(): exponent = jnp.exp(scores - peak_score)  7.03 us
  transfers between devices with their start and end apart: 4, of which 3 were waited for; matrix products, arithmetic and copies ran while one was open for 6% of the time, Pallas kernels for 0%

commit v1 on v0

--- a/solution.py
+++ b/solution.py
@@ -9,6 +9,13 @@
 COUPLING_DIM = 32
 epsilon = 1e-05
 mask_fill = 1000000000.0
+
+
+def swap_blocks(x, name, split, join):
+    size = lax.axis_size(name)
+    tiles = jnp.stack(jnp.split(x, size, axis=split), axis=0)
+    tiles = lax.all_to_all(tiles, name, split_axis=0, concat_axis=0)
+    return jnp.concatenate(tiles, axis=join)
 
 
 def layer_norm(values):
@@ -146,7 +153,7 @@
         second_factor_matrix,
     )
     grouped = homolog_embedding.reshape(shard_rows, seq_count, owned_columns, channel_width)
-    flat_block = lax.all_to_all(grouped, "seq", split_axis=1, concat_axis=0, tiled=True)[:, 0]
+    flat_block = swap_blocks(grouped, "seq", 1, 0)[:, 0]
     after_trans, left_proj, right_proj = column_delta(
         flat_block, row_present_flags, attention_weights
     )

time: 130 us -> 139 us (1.069)
  local copies, waits for them, and re-layouts: 16.8 us -> 26 us
    unnamed x34 -> x49, local copies, waits for them, and re-layouts: 5.11 us -> 13.6 us
where the time goes in v1:
time: 139 us
  waiting for transfers between devices  32.4 us (23%)
  local copies, waits for them, and re-layouts  26 us (19%)
  matrix products  25.8 us (19%)
  blocking collectives  19.3 us (14%)
  starting transfers between devices  14.9 us (11%)
  between operations  14.4 us (10%)
  other arithmetic  5.77 us (4%)
    unnamed x49, local copies, waits for them, and re-layouts  13.6 us
    all_to_all x1, waiting for transfers between devices, per_device(): lax.all_to_all(alignment_columns, 'seq', split_axis=0, concat_axis=1, til...  12.2 us
    all_to_all x1, waiting for transfers between devices, swap_blocks(): tiles = lax.all_to_all(tiles, name, split_axis=0, concat_axis=0)  12.2 us
    all_to_all x1, blocking collectives, per_device(): lax.all_to_all(left_column_set, 'seq', split_axis=0, concat_axis=1, tiled...  10.9 us
    all_gather x1, blocking collectives, per_device(): left_wide = lax.all_gather(left_home, 'res', axis=1, tiled=True)  8.43 us
    all_to_all x1, waiting for transfers between devices, per_device(): lax.all_to_all(left_wide, 'seq', split_axis=1, concat_axis=0, tiled=True)  7.96 us
    convert_element_type x1, local copies, waits for them, and re-layouts, pair_block_update(): outer = jnp.einsum('sic,sje->ijce', left_rows, right_full, preferred_elem...  7.69 us
    all_to_all x1, starting transfers between devices, swap_blocks(): tiles = lax.all_to_all(tiles, name, split_axis=0, concat_axis=0)  7.55 us
  transfers between devices with their start and end apart: 4, of which 3 were waited for; matrix products, arithmetic and copies ran while one was open for 6% of the time, Pallas kernels for 0%

profile of v1, /device:TPU:0, one launch (start us, length us, event | category | flops | bytes accessed | tf_op | source)
XLA Modules:
  0.0 138.5 jit_solution(10299040306327371390)
XLA Ops:
  7.2 1.4 %copy.168 = bf16[16,64,256]{2,0,1:T(8,128)(2,1)S(1)} copy(bf16[16,64,256]{2,1,0:T(8,128)(2,1)} %param.17) | data formatting | bytes 1048576 | tf_op args[0]
  8.6 0.6 constant_dynamic-update-slice_fusion.15
  9.2 0.6 constant_dynamic-update-slice_fusion.14
  9.8 0.6 constant_dynamic-update-slice_fusion.13
  10.4 0.6 constant_dynamic-update-slice_fusion.12
  11.0 0.6 constant_dynamic-update-slice_fusion.11
  11.7 0.6 constant_dynamic-update-slice_fusion.10
  12.3 0.6 constant_dynamic-update-slice_fusion.9
  12.9 0.6 constant_dynamic-update-slice_fusion.8
  13.5 0.6 constant_dynamic-update-slice_fusion.7
  14.1 0.6 constant_dynamic-update-slice_fusion.6
  14.7 0.6 constant_dynamic-update-slice_fusion.5
  15.4 0.6 constant_dynamic-update-slice_fusion.4
  16.0 0.6 constant_dynamic-update-slice_fusion.3
  16.6 0.6 constant_dynamic-update-slice_fusion.2
  17.2 0.6 constant_dynamic-update-slice_fusion.1
  17.8 0.6 constant_dynamic-update-slice_fusion
  18.5 7.5 %all-to-all-start = ((bf16[16,16,1,4,256]{4,1,3,2,0:T(8,128)(2,1)}), bf16[16,16,1,4,256]{4,1,3,2,0:T(8,128)(2,1)S(1)}, u32[]{:S(2)}, u32[]{:S(2)}) async-start(bf16[16,16,1,4,256]{4,1,3,2,0:T(8,128)(2,1)} %constant_dynamic-update-slice_fusion), calls=%async_computation | async-start | bytes 1048576 | tf_op jit(solution)/shard_map/all_to_all | solution.py:17
  26.1 0.7 convert_element_type.110
  26.7 1.3 convert_reduce_fusion.3
  28.1 12.2 %all-to-all-done = bf16[16,16,1,4,256]{4,1,3,2,0:T(8,128)(2,1)S(1)} async-done(((bf16[16,16,1,4,256]{4,1,3,2,0:T(8,128)(2,1)}), bf16[16,16,1,4,256]{4,1,3,2,0:T(8,128)(2,1)S(1)}, u32[]{:S(2)}, u32[]{:S(2)}) %all-to-all-start) | async-done | bytes 524320 | tf_op jit(solution)/shard_map/all_to_all | solution.py:17
  40.7 0.4 multiply_reduce_fusion
  41.3 0.3 copy.179
  41.7 0.3 multiply_convert_fusion
  42.0 0.3 fusion.14
  42.4 1.1 convolution_convert_fusion
  43.5 0.3 convolution_convert_fusion.1
  43.9 7.0 %fusion.73 = (f32[4,8,256]{2,1,0:T(8,128)S(1)}, f32[4,8,256,256]{2,3,1,0:T(8,128)}) fusion(f32[256]{0:T(256)S(1)} %get-tuple-element.43, bf16[256,4,8,32]{0,3,2,1:T(8,128)(2,1)S(1)} %bitcast.188, bf16[256,4,8,32]{0,3,2,1:T(8,128)(2,1)} %bitcast.189), kind=kOutput, calls=%fused_computation.131 | convolution fusion | flops 140509440 | bytes 9470976 | tf_op jit(solution)/shard_map/sub | solution.py:59
  50.9 5.3 %fusion.5 = f32[4,8,32,256]{3,2,1,0:T(8,128)} fusion(bf16[256,4,8,32]{0,3,2,1:T(8,128)(2,1)S(1)} %bitcast.187, f32[4,8,256,256]{2,3,1,0:T(8,128)} %get-tuple-element.47, f32[4,8,256]{2,1,0:T(8,128)S(1)} %get-tuple-element.46), kind=kOutput, calls=%fused_computation.8 | convolution fusion | flops 138412032 | bytes 9994240 | tf_op jit(solution)/shard_map/khst,tkhd->skhd/dot_general | solution.py:61
  56.2 1.6 %copy.177 = f32[256,4,256]{2,0,1:T(8,128)S(1)} copy(f32[256,4,256]{0,2,1:T(8,128)} %bitcast.185) | data formatting | bytes 2097152 | tf_op jit(solution)/shard_map/reshape | solution.py:62
  57.8 1.4 %convert_reduce_fusion = (f32[256,4]{0,1:T(4,128)S(1)}, bf16[256,4,256]{0,2,1:T(8,128)(2,1)}) fusion(f32[256,4,256]{0,2,1:T(8,128)S(1)} %copy.179, bf16[256,256]{1,0:T(8,128)(2,1)S(1)} %copy-done.6, f32[256,4,256]{2,0,1:T(8,128)S(1)} %copy.177, bf16[256,4,256]{2,0,1:T(8,128)(2,1)S(1)} %multiply_convert_fusion, bf16[256,256]{1,0:T(8,128)(2,1)S(1)} %copy-done.7), kind=kOutput, calls=%fused_computation.12 | convolution fusion | flops 270793728 | bytes 3411968 | tf_op jit(solution)/shard_map/dot_general | solution.py:65
  59.2 1.2 fusion.29
  60.5 2.7 %convert_reduce_fusion.1 = (f32[256,4]{0,1:T(4,128)S(1)}, bf16[256,4,256]{0,2,1:T(8,128)(2,1)S(1)}) fusion(bf16[1024,256]{1,0:T(8,128)(2,1)S(1)} %copy-done, bf16[256,4,256]{0,2,1:T(8,128)(2,1)} %get-tuple-element.49, bf16[256,1024]{1,0:T(8,128)(2,1)} %param.26, f32[256,4]{0,1:T(4,128)S(1)} %add_rsqrt_fusion.2, f32[256,4]{0,1:T(4,128)S(1)} %broadcast_multiply_fusion.2), kind=kOutput, calls=%fused_computation.22 | convolution fusion | flops 1078197248 | bytes 2109440 | tf_op jit(solution)/shard_map/dot_general | solution.py:73
  63.4 0.9 fusion.27
  65.0 10.9 %all_to_all.59 = bf16[16,2,1024]{2,1,0:T(2,128)(2,1)S(1)} all-to-all(bf16[16,2,1024]{2,1,0:T(2,128)(2,1)S(1)} %reshape.146), channel_id=1, replica_groups=mesh['seq'=16,'res'=2] {'seq'}, dimensions={0} | all-to-all | bytes 131072 | tf_op jit(solution)/shard_map/all_to_all | solution.py:168
  76.1 8.4 %all_gather.7 = bf16[16,128,32]{2,0,1:T(8,128)(2,1)S(1)} all-gather(bf16[16,64,32]{2,0,1:T(8,128)(2,1)S(1)} %bitcast.184), channel_id=1, replica_groups=mesh['seq'=16,'res'=2] {'res'}, dimensions={1}, use_global_device_ids=true | all-gather | bytes 196608 | tf_op jit(solution)/shard_map/all_gather | solution.py:171
  84.6 1.2 reshape.148
  85.7 3.5 %all-to-all-start.3 = ((bf16[16,2,2048]{2,1,0:T(2,128)(2,1)}), bf16[16,2,2048]{2,1,0:T(2,128)(2,1)S(1)}, u32[]{:S(2)}, u32[]{:S(2)}) async-start(bf16[16,2,2048]{2,1,0:T(2,128)(2,1)} %reshape.148), calls=%async_computation.3 | async-start | bytes 262144 | tf_op jit(solution)/shard_map/all_to_all | solution.py:172
  89.3 1.1 copy.182
  90.3 8.0 %all-to-all-done.3 = bf16[16,2,2048]{2,1,0:T(2,128)(2,1)S(1)} async-done(((bf16[16,2,2048]{2,1,0:T(2,128)(2,1)}), bf16[16,2,2048]{2,1,0:T(2,128)(2,1)S(1)}, u32[]{:S(2)}, u32[]{:S(2)}) %all-to-all-start.3) | async-done | bytes 131104 | tf_op jit(solution)/shard_map/all_to_all | solution.py:172
  98.3 3.8 %all-to-all-start.1 = ((bf16[256,4,256]{2,1,0:T(4,128)(2,1)}), bf16[256,4,256]{2,1,0:T(4,128)(2,1)S(1)}, u32[]{:S(2)}, u32[]{:S(2)}) async-start(bf16[256,4,256]{2,1,0:T(4,128)(2,1)} %copy.182), calls=%async_computation.1 | async-start | bytes 1048576 | tf_op jit(solution)/shard_map/all_to_all | solution.py:167
  102.1 0.7 convert_multiply_fusion
  103.9 12.2 %all-to-all-done.1 = bf16[256,4,256]{2,1,0:T(4,128)(2,1)S(1)} async-done(((bf16[256,4,256]{2,1,0:T(4,128)(2,1)}), bf16[256,4,256]{2,1,0:T(4,128)(2,1)S(1)}, u32[]{:S(2)}, u32[]{:S(2)}) %all-to-all-start.1) | async-done | bytes 524320 | tf_op jit(solution)/shard_map/all_to_all | solution.py:167
  116.2 1.0 copy.195
  117.2 4.4 %convert_bitcast_fusion = bf16[8,64,32,32]{2,3,0,1:T(8,128)(2,1)} fusion(bf16[256,64,32]{0,2,1:T(8,128)(2,1)} %all-gather.2.cloned.1.call-done, bf16[64]{0:T(256)(128)(2,1)S(1)} %get-tuple-element.45, bf16[256,8,32]{0,2,1:T(8,128)(2,1)S(1)} %copy.192), kind=kOutput, calls=%fused_computation.5 | convolution fusion | flops 271056896 | bytes 2228352 | tf_op jit(solution)/shard_map/while/body/eval_jaxpr/sic,sje->ijce/dot_general | solution.py:96
  121.7 7.7 %copy.193 = bf16[8,64,32,32]{1,3,2,0:T(8,128)(2,1)S(1)} copy(bf16[8,64,32,32]{2,3,0,1:T(8,128)(2,1)} %convert_bitcast_fusion) | data formatting | bytes 2097152 | tf_op jit(solution)/shard_map/while/body/eval_jaxpr/convert_element_type | solution.py:98
  129.4 0.8 fusion.80
  130.5 1.1 fusion.26
  (61 shorter events, 3.3 us)
Async XLA Ops:
  7.2 53.3 %copy-start = (bf16[1024,256]{1,0:T(8,128)(2,1)S(1)}, bf16[1024,256]{1,0:T(8,128)(2,1)}, u32[]{:S(2)}) copy-start(bf16[1024,256]{1,0:T(8,128)(2,1)} %param.27) | copy-start | bytes 1572868
  12.3 29.7 %copy-start.1 = (bf16[256,256]{1,0:T(8,128)(2,1)S(1)}, bf16[256,256]{1,0:T(8,128)(2,1)}, u32[]{:S(2)}) copy-start(bf16[256,256]{1,0:T(8,128)(2,1)} %param.21) | copy-start | bytes 393220
  18.5 23.9 %copy-start.2 = (bf16[256,256]{1,0:T(8,128)(2,1)S(1)}, bf16[256,256]{1,0:T(8,128)(2,1)}, u32[]{:S(2)}) copy-start(bf16[256,256]{1,0:T(8,128)(2,1)} %param.22) | copy-start | bytes 393220
  18.5 21.8 %all-to-all-start = ((bf16[16,16,1,4,256]{4,1,3,2,0:T(8,128)(2,1)}), bf16[16,16,1,4,256]{4,1,3,2,0:T(8,128)(2,1)S(1)}, u32[]{:S(2)}, u32[]{:S(2)}) async-start(bf16[16,16,1,4,256]{4,1,3,2,0:T(8,128)(2,1)} %constant_dynamic-update-slice_fusion), calls=%async_computation | async-start | bytes 1048576 | tf_op jit(solution)/shard_map/all_to_all | solution.py:17
  26.0 91.2 %all-gather.2.cloned.1.call-start = ((), (), s32[]{:S(2)}) async-start(), calls=%async_computation.4 | async-start | bytes 1114112 | tf_op jit(solution)/shard_map/all_gather | solution.py:170
  40.5 3.0 %copy-start.3 = (bf16[256,256]{1,0:T(8,128)(2,1)S(1)}, bf16[256,256]{1,0:T(8,128)(2,1)}, u32[]{:S(2)}) copy-start(bf16[256,256]{1,0:T(8,128)(2,1)} %param.23) | copy-start | bytes 393220
  50.9 6.9 %copy-start.6 = (bf16[256,256]{1,0:T(8,128)(2,1)S(1)}, bf16[256,256]{1,0:T(8,128)(2,1)}, u32[]{:S(2)}) copy-start(bf16[256,256]{1,0:T(8,128)(2,1)} %param.25) | copy-start | bytes 393220
  50.9 6.9 %copy-start.7 = (bf16[256,256]{1,0:T(8,128)(2,1)S(1)}, bf16[256,256]{1,0:T(8,128)(2,1)}, u32[]{:S(2)}) copy-start(bf16[256,256]{1,0:T(8,128)(2,1)} %param.24) | copy-start | bytes 393220
  59.2 4.1 %copy-start.11 = (bf16[256,32]{0,1:T(8,128)(2,1)S(1)}, bf16[256,32]{0,1:T(8,128)(2,1)}, u32[]{:S(2)}) copy-start(bf16[256,32]{0,1:T(8,128)(2,1)} %param.29) | copy-start | bytes 49156
  59.2 5.0 %copy-start.12 = (bf16[256,32]{0,1:T(8,128)(2,1)S(1)}, bf16[256,32]{0,1:T(8,128)(2,1)}, u32[]{:S(2)}) copy-start(bf16[256,32]{0,1:T(8,128)(2,1)} %param.28) | copy-start | bytes 49156
  63.1 38.9 %copy-start.4 = (s32[128]{0:T(128)S(1)}, s32[128]{0:T(128)}, u32[]{:S(2)}) copy-start(s32[128]{0:T(128)} %param.20) | copy-start | bytes 1540
  85.7 12.5 %all-to-all-start.3 = ((bf16[16,2,2048]{2,1,0:T(2,128)(2,1)}), bf16[16,2,2048]{2,1,0:T(2,128)(2,1)S(1)}, u32[]{:S(2)}, u32[]{:S(2)}) async-start(bf16[16,2,2048]{2,1,0:T(2,128)(2,1)} %reshape.148), calls=%async_computation.3 | async-start | bytes 262144 | tf_op jit(solution)/shard_map/all_to_all | solution.py:172
  98.3 17.8 %all-to-all-start.1 = ((bf16[256,4,256]{2,1,0:T(4,128)(2,1)}), bf16[256,4,256]{2,1,0:T(4,128)(2,1)S(1)}, u32[]{:S(2)}, u32[]{:S(2)}) async-start(bf16[256,4,256]{2,1,0:T(4,128)(2,1)} %copy.182), calls=%async_computation.1 | async-start | bytes 1048576 | tf_op jit(solution)/shard_map/all_to_all | solution.py:167
  121.6 7.7 %copy-start.5 = (bf16[1024,128]{1,0:T(8,128)(2,1)S(1)}, bf16[1024,128]{1,0:T(8,128)(2,1)}, u32[]{:S(2)}) copy-start(bf16[1024,128]{1,0:T(8,128)(2,1)} %param.30) | copy-start | bytes 786436
  121.6 7.7 %copy-start.8 = (bf16[8,64,128]{2,1,0:T(8,128)(2,1)S(1)}, bf16[8,64,128]{2,1,0:T(8,128)(2,1)}, u32[]{:S(2)}) copy-start(bf16[8,64,128]{2,1,0:T(8,128)(2,1)} %param.18) | copy-start | bytes 393220
  121.6 7.7 %copy-start.13 = (f32[128]{0:T(128)S(1)}, f32[128]{0:T(128)}, u32[]{:S(2)}) copy-start(f32[128]{0:T(128)} %param.31) | copy-start | bytes 1540
  121.6 8.9 %copy-start.9 = (bf16[512,128]{1,0:T(8,128)(2,1)S(1)}, bf16[512,128]{1,0:T(8,128)(2,1)}, u32[]{:S(2)}) copy-start(bf16[512,128]{1,0:T(8,128)(2,1)} %param.33) | copy-start | bytes 393220
  121.6 8.9 %copy-start.10 = (bf16[128,512]{1,0:T(8,128)(2,1)S(1)}, bf16[128,512]{1,0:T(8,128)(2,1)}, u32[]{:S(2)}) copy-start(bf16[128,512]{1,0:T(8,128)(2,1)} %param.32) | copy-start | bytes 393220
Sparse Core Ops, SparseCore 0:
  64.4 37.4 all-gather.1
